TPU v7x, 128 devices: a whole 4x4x4 slice. The times are simulated.
128 devices in a mesh: seq: 16 (over z_hi, y, core), head: 8 (over x, z_lo).
Axes of the slice: x: 4, y: 4, z: 4 (z_hi: 2, z_lo: 2; z = z_hi * 2 + z_lo), core: 2. Of those that a mesh axis runs over, the one named last changes fastest.
Arguments:
- latent: bfloat16 [16, 1024, 2048], P('seq', None, 'head'), may hold values from -6 to 6
- modulation: float32 [9, 2048], replicated, may hold values from -3 to 3
- spatial_qkv: bfloat16 [3, 2048, 2048], P(None, None, 'head')
- spatial_out: bfloat16 [2048, 2048], P('head'), may hold values from -0.125 to 0.125
- temporal_qkv: bfloat16 [3, 2048, 2048], P(None, None, 'head')
- temporal_out: bfloat16 [2048, 2048], P('head'), may hold values from -0.125 to 0.125
- hidden_weight: bfloat16 [2048, 8192], P(None, 'head'), may hold values from -0.125 to 0.125
- output_weight: bfloat16 [8192, 2048], P('head'), may hold values from -0.0625 to 0.0625
Outputs:
- block_out: bfloat16 [16, 1024, 2048], P(None, 'seq', 'head')
All inputs are finite; a program needn't handle non-finite values.
Results may differ from a plain program's by a relative error of at most 0.009.
Values may be sent and summed in bfloat16 or wider, within the bound.
A program may use at most 128 MiB of HBM per device.

v0:
```python
import jax
import jax.numpy as jnp
from jax import lax
from jax.sharding import PartitionSpec as P

HD = 64


def split_up(shard, dim, devices):
    lengths = shard.shape
    blocks = shard.reshape(*lengths[:dim], devices, lengths[dim] // devices, *lengths[dim + 1 :])
    return jnp.moveaxis(blocks, dim, 0)


def sum_at_owner(shard, axis, dim):
    devices = lax.axis_size(axis)
    blocks = lax.all_to_all(split_up(shard, dim, devices), axis, 0, 0, tiled=True)
    return jnp.sum(blocks.astype(jnp.float32), axis=0)


def layer_norm(values):
    average = jnp.mean(values, axis=-1, keepdims=True)
    centred = values - average
    variance = jnp.mean(centred * centred, axis=-1, keepdims=True)
    return centred * lax.rsqrt(variance + 1e-06)


def modulate(stream, modulation, offset):
    normed = layer_norm(stream.astype(jnp.float32))
    return (normed * (1.0 + modulation[offset + 1]) + modulation[offset]).astype(jnp.bfloat16)


def attend(query, keys, values):
    scores = jnp.einsum(
        "glhd,gmhd->ghlm", query, keys, preferred_element_type=jnp.float32
    ) * HD ** (-0.5)
    attn_weights = jax.nn.softmax(scores, axis=-1).astype(jnp.bfloat16)
    return jnp.einsum(
        "ghlm,gmhd->glhd", attn_weights, values, preferred_element_type=jnp.float32
    ).astype(jnp.bfloat16)


def project_three(normed, weights):
    return [
        jnp.dot(normed, weights[member], preferred_element_type=jnp.float32).astype(jnp.bfloat16)
        for member in range(3)
    ]


def column_adder(columns, portion):
    return jnp.dot(portion, columns, preferred_element_type=jnp.float32)


def per_device(
    latent,
    modulation,
    spatial_qkv,
    spatial_out,
    temporal_qkv,
    temporal_out,
    hidden_weight,
    output_weight,
):
    width_local = latent.shape[2]
    heads_local = width_local // HD
    anchor = lax.axis_index("head") * width_local
    local_rows = lax.dynamic_slice_in_dim(modulation, anchor, width_local, 1)
    full_spatial = lax.all_gather(latent, "head", axis=2, tiled=True)
    normed = modulate(full_spatial, modulation, 0)
    frames_local = latent.shape[0]
    patches = latent.shape[1]
    query, keys, values = [
        member.reshape(frames_local, patches, heads_local, HD)
        for member in project_three(normed, spatial_qkv)
    ]
    spatial = lax.map(
        lambda triple: attend(triple[0][None], triple[1][None], triple[2][None])[0],
        (query, keys, values),
    )
    spatial = spatial.reshape(frames_local, patches, width_local)
    columns = lax.all_to_all(spatial_out, "head", split_axis=1, concat_axis=0, tiled=True)
    reduced = column_adder(columns, lax.all_gather(spatial, "head", axis=2, tiled=True))
    stream_one = (latent.astype(jnp.float32) + local_rows[2] * reduced).astype(jnp.bfloat16)
    stream_temporal = lax.all_to_all(stream_one, "seq", split_axis=1, concat_axis=0, tiled=True)
    full_temporal = lax.all_gather(stream_temporal, "head", axis=2, tiled=True)
    normed = modulate(full_temporal, modulation, 3)
    query, keys, values = project_three(normed, temporal_qkv)
    frames = stream_temporal.shape[0]
    patches_local = stream_temporal.shape[1]

    def to_groups(tensor):
        return jnp.transpose(tensor.reshape(frames, patches_local, heads_local, HD), (1, 0, 2, 3))

    temporal = attend(to_groups(query), to_groups(keys), to_groups(values))
    temporal = jnp.transpose(temporal, (1, 0, 2, 3)).reshape(frames, patches_local, width_local)
    columns = lax.all_to_all(temporal_out, "head", split_axis=1, concat_axis=0, tiled=True)
    reduced = column_adder(columns, lax.all_gather(temporal, "head", axis=2, tiled=True))
    stream_two = (stream_temporal.astype(jnp.float32) + local_rows[5] * reduced).astype(
        jnp.bfloat16
    )
    full_two = lax.all_gather(stream_two, "head", axis=2, tiled=True)
    normed = modulate(full_two, modulation, 6)
    pre_act = jnp.dot(normed, hidden_weight, preferred_element_type=jnp.float32)
    hidden = jax.nn.gelu(pre_act, approximate=True).astype(jnp.bfloat16)
    partial_sums = jnp.dot(hidden, output_weight, preferred_element_type=jnp.float32)
    reduced = sum_at_owner(partial_sums.astype(jnp.bfloat16), "head", 2)
    return (stream_two.astype(jnp.float32) + local_rows[8] * reduced).astype(jnp.bfloat16)


def solution(mesh):
    in_specs = (
        P("seq", None, "head"),
        P(),
        P(None, None, "head"),
        P("head", None),
        P(None, None, "head"),
        P("head", None),
        P(None, "head"),
        P("head", None),
    )
    out_specs = P(None, "seq", "head")
    return jax.shard_map(
        per_device, mesh=mesh, in_specs=in_specs, out_specs=out_specs, check_vma=False
    )
```

profile of v0, /device:TPU:8, one launch (start us, length us, event | category | flops | bytes accessed | tf_op | source)
XLA Modules:
  0.0 685.8 jit_solution(7628114898617417352)
XLA Ops:
  6.5 0.7 all-gather.6.cloned.1.call-update
  7.3 1.1 slice_add_fusion
  8.4 99.1 %all-gather.6.cloned.1.call-done = bf16[1,1024,2048]{2,1,0:T(8,128)(2,1)} async-done(((bf16[1,1024,256]{2,1,0:T(8,128)(2,1)}), bf16[1,1024,2048]{2,1,0:T(8,128)(2,1)}) %all-gather.6.cloned.1.call-update) | async-done | bytes 4194320 | tf_op jit(solution)/shard_map/all_gather | solution.py:68
  107.6 3.0 convert_reduce_fusion.2
  110.5 0.5 copy-done
  111.0 1.2 fusion.19
  112.3 1.9 fusion.33
  114.2 1.3 convolution_convert_fusion.6
  115.5 1.3 convolution_convert_fusion.5
  116.8 1.3 convolution_convert_fusion.4
  118.1 5.2 fusion.130
  123.3 8.1 %fusion.136 = f32[4,1024,1024]{1,2,0:T(8,128)} fusion(bf16[1024,4,64]{0,2,1:T(8,128)(2,1)S(1)} %bitcast.142, bf16[1024,4,64]{0,2,1:T(8,128)(2,1)S(1)} %bitcast.144), kind=kOutput, calls=%fused_computation.124 | convolution fusion | flops 536870912 | bytes 17825792 | tf_op jit(solution)/shard_map/while/body/eval_jaxpr/glhd,gmhd->ghlm/dot_general | solution.py:34
  131.4 16.0 %fusion.69 = bf16[4,64,1024]{2,1,0:T(8,128)(2,1)} fusion(bf16[1024,4,64]{0,2,1:T(8,128)(2,1)S(1)} %bitcast.162, f32[4,1024]{1,0:T(4,128)S(1)} %fusion.130, f32[4,1024,1024]{1,2,0:T(8,128)} %fusion.136), kind=kOutput, calls=%fused_computation.78 | convolution fusion | flops 558109696 | bytes 17842176 | tf_op jit(solution)/shard_map/while/body/eval_jaxpr/ghlm,gmhd->glhd/dot_general | solution.py:38
  147.4 1.3 copy.43
  148.7 6.0 all-to-all-start
  154.8 0.9 fusion.129
  155.6 21.3 %all-to-all-done = bf16[256,8,256]{0,2,1:T(8,128)(2,1)S(1)} async-done(((bf16[256,8,256]{0,2,1:T(8,128)(2,1)}), bf16[256,8,256]{0,2,1:T(8,128)(2,1)S(1)}, u32[]{:S(2)}, u32[]{:S(2)}) %all-to-all-start) | async-done | bytes 1048608 | tf_op jit(solution)/shard_map/all_to_all | solution.py:81
  177.0 0.5 copy.44
  177.5 71.1 %all-gather.8.cloned.1.call-done = bf16[1,1024,2048]{1,2,0:T(8,128)(2,1)} async-done(((bf16[1,1024,256]{1,2,0:T(8,128)(2,1)}), bf16[1,1024,2048]{1,2,0:T(8,128)(2,1)}) %all-gather.8.cloned.1.call-update) | async-done | bytes 4194320 | tf_op jit(solution)/shard_map/all_gather | solution.py:82
  248.6 3.5 fusion.65
  252.1 0.8 copy.91
  252.9 0.5 broadcast.127
  253.4 3.8 reduce.6
  257.4 15.9 %all_to_all.55 = bf16[16,2,8192]{2,1,0:T(2,128)(2,1)S(1)} all-to-all(bf16[16,2,8192]{2,1,0:T(2,128)(2,1)S(1)} %reshape.181), channel_id=1, replica_groups=mesh['seq'=16,'head'=8] {'seq'}, dimensions={0} | all-to-all | bytes 1048576 | tf_op jit(solution)/shard_map/all_to_all | solution.py:84
  273.2 0.5 reshape.182
  273.8 0.9 copy.55
  274.9 94.6 %all-gather.10.cloned.1.call-done = bf16[16,64,2048]{2,1,0:T(8,128)(2,1)} async-done(((bf16[16,64,256]{2,1,0:T(8,128)(2,1)}), bf16[16,64,2048]{2,1,0:T(8,128)(2,1)}) %all-gather.10.cloned.1.call-update) | async-done | bytes 4194320 | tf_op jit(solution)/shard_map/all_gather | solution.py:85
  369.5 3.0 convert_reduce_fusion.1
  372.9 1.2 fusion.15
  374.2 3.0 convolution_convert_fusion.1
  377.5 4.2 convolution_convert_fusion.2
  382.2 5.0 convolution_convert_fusion.3
  387.2 2.2 reshape.170
  389.4 3.3 fusion.131
  392.7 2.5 fusion.54
  395.2 0.5 copy.50
  395.7 1.5 reshape.173
  397.4 24.8 %all_to_all.56 = bf16[256,8,256]{2,0,1:T(8,128)(2,1)S(1)} all-to-all(bf16[256,8,256]{2,0,1:T(8,128)(2,1)S(1)} %bitcast.138), channel_id=1, replica_groups=mesh['seq'=16,'head'=8] {'head'}, dimensions={1} | all-to-all | bytes 2097152 | tf_op jit(solution)/shard_map/all_to_all | solution.py:96
  422.2 74.8 %all-gather.12.cloned.1.call-done = bf16[16,64,2048]{2,1,0:T(8,128)(2,1)} async-done(((bf16[16,64,256]{2,1,0:T(8,128)(2,1)}), bf16[16,64,2048]{2,1,0:T(8,128)(2,1)}) %all-gather.12.cloned.1.call-update) | async-done | bytes 4194320 | tf_op jit(solution)/shard_map/all_gather | solution.py:97
  497.0 4.2 fusion.68
  501.3 100.4 %all-gather.14.cloned.1.call-done = bf16[16,64,2048]{2,1,0:T(8,128)(2,1)} async-done(((bf16[16,64,256]{2,1,0:T(8,128)(2,1)}), bf16[16,64,2048]{2,1,0:T(8,128)(2,1)}) %all-gather.14.cloned.1.call-update) | async-done | bytes 4194320 | tf_op jit(solution)/shard_map/all_gather | solution.py:101
  601.7 3.0 convert_reduce_fusion
  605.2 1.2 fusion.11
  606.4 15.3 %fusion.45 = bf16[16,64,2048]{2,1,0:T(8,128)(2,1)} fusion(bf16[1024,2048]{1,0:T(8,128)(2,1)} %param.15, bf16[16,64,2048]{2,1,0:T(8,128)(2,1)} %all-gather.14.cloned.1.call-done, bf16[2048,1024]{1,0:T(8,128)(2,1)} %param.14, f32[2048]{0:T(1024)S(1)} %bitcast.152, f32[2048]{0:T(1024)S(1)} %bitcast.151, f32[16,64]{1,0:T(8,128)S(1)} %add_rsqrt_fusion, ...), kind=kOutput, calls=%fused_computation.54 | convolution fusion | flops 8614051840 | bytes 16801792 | tf_op jit(solution)/shard_map/dot_general | solution.py:105
  621.7 2.8 copy.89
  624.5 52.6 %all_to_all.57 = bf16[8,16,64,256]{3,2,1,0:T(8,128)(2,1)S(1)} all-to-all(bf16[8,16,64,256]{3,2,1,0:T(8,128)(2,1)S(1)} %bitcast.133), channel_id=1, replica_groups=mesh['seq'=16,'head'=8] {'head'}, dimensions={0} | all-to-all | bytes 8388608 | tf_op jit(solution)/shard_map/all_to_all | solution.py:17
  677.1 0.7 convert_reduce_fusion.3
  678.1 0.9 add_convert_fusion
  (36 shorter events, 2.8 us)
Async XLA Ops:
  6.5 101.0 %all-gather.6.cloned.1.call-start = ((), (), s32[]{:S(2)}) async-start(), calls=%async_computation.4 | async-start | bytes 4718592 | tf_op jit(solution)/shard_map/all_gather | solution.py:68
  7.3 241.3 %all-gather.8.cloned.1.call-start = ((), (), s32[]{:S(2)}) async-start(), calls=%async_computation.5 | async-start | bytes 4718592 | tf_op jit(solution)/shard_map/all_gather | solution.py:82
  107.6 3.4 copy-start
  112.3 1.9 copy-start.8
  131.4 16.0 %copy-start.5 = (bf16[256,2048]{1,0:T(8,128)(2,1)S(1)}, bf16[256,2048]{1,0:T(8,128)(2,1)}, u32[]{:S(2)}) copy-start(bf16[256,2048]{1,0:T(8,128)(2,1)} %param.11) | copy-start | bytes 3145732
  147.4 101.2 %copy-start.7 = (bf16[1,1024,256]{2,1,0:T(8,128)(2,1)S(1)}, bf16[1,1024,256]{2,1,0:T(8,128)(2,1)}, u32[]{:S(2)}) copy-start(bf16[1,1024,256]{2,1,0:T(8,128)(2,1)} %param.8) | copy-start | bytes 1572868
  148.7 28.2 %all-to-all-start = ((bf16[256,8,256]{0,2,1:T(8,128)(2,1)}), bf16[256,8,256]{0,2,1:T(8,128)(2,1)S(1)}, u32[]{:S(2)}, u32[]{:S(2)}) async-start(bf16[256,8,256]{0,2,1:T(8,128)(2,1)} %bitcast.14), calls=%async_computation | async-start | bytes 2097152 | tf_op jit(solution)/shard_map/all_to_all | solution.py:81
  154.7 214.7 %all-gather.10.cloned.1.call-start = ((), (), s32[]{:S(2)}) async-start(), calls=%async_computation.6 | async-start | bytes 4718592 | tf_op jit(solution)/shard_map/all_gather | solution.py:85
  274.7 222.4 %all-gather.12.cloned.1.call-start = ((), (), s32[]{:S(2)}) async-start(), calls=%async_computation.7 | async-start | bytes 4718592 | tf_op jit(solution)/shard_map/all_gather | solution.py:97
  369.5 3.4 copy-start.1
  395.2 2.1 copy-start.6
  395.2 101.8 %copy-start.3 = (bf16[1,1024,256]{2,1,0:T(8,128)(2,1)S(1)}, bf16[1,1024,256]{2,1,0:T(8,128)(2,1)}, u32[]{:S(2)}) copy-start(bf16[1,1024,256]{2,1,0:T(8,128)(2,1)} %copy.55) | copy-start | bytes 1572868
  397.2 204.5 %all-gather.14.cloned.1.call-start = ((), (), s32[]{:S(2)}) async-start(), calls=%async_computation.8 | async-start | bytes 4718592 | tf_op jit(solution)/shard_map/all_gather | solution.py:101
  601.7 3.4 copy-start.2
  677.1 1.0 copy-start.4
Sparse Core Ops, SparseCore 0:
  8.9 98.6 all-gather.5
  147.5 101.0 all-gather.7
  274.8 94.6 all-gather.9
  397.3 99.6 all-gather.11
  501.4 100.2 all-gather.13
where the time goes:
time: 696 us; the launch traced here: 686 us
  waiting for transfers between devices  462 us (66%)
  blocking collectives  93.3 us (13%)
  matrix products  74.2 us (11%)
  other arithmetic  21.1 us (3%)
  local copies, waits for them, and re-layouts  15.2 us (2%)
  between operations  13.6 us (2%)
    all_gather x1, waiting for transfers between devices, per_device(): full_two = lax.all_gather(stream_two, 'head', axis=2, tiled=True)  100 us
    all_gather x1, waiting for transfers between devices, per_device(): full_spatial = lax.all_gather(latent, 'head', axis=2, tiled=True)  99.1 us
    all_gather x1, waiting for transfers between devices, per_device(): full_temporal = lax.all_gather(stream_temporal, 'head', axis=2, tiled=True)  94.6 us
    all_gather x1, waiting for transfers between devices, per_device(): lax.all_gather(temporal, 'head', axis=2, tiled=True)  74.8 us
    all_gather x1, waiting for transfers between devices, per_device(): lax.all_gather(spatial, 'head', axis=2, tiled=True)  71.1 us
    all_to_all x1, blocking collectives, sum_at_owner(): lax.all_to_all(split_up(shard, dim, devices), axis, 0, 0, tiled=True)  52.6 us
    all_to_all x1, blocking collectives, per_device(): lax.all_to_all(temporal_out, 'head', split_axis=1, concat_axis=0, tiled=T...  24.8 us
    all_to_all x1, waiting for transfers between devices, per_device(): lax.all_to_all(spatial_out, 'head', split_axis=1, concat_axis=0, tiled=True)  21.3 us
  transfers between devices with their start and end apart: 6, of which 6 were waited for; matrix products, arithmetic and copies ran while one was open for 1% of the time, Pallas kernels for 0%

commit v1 on v0

--- a/solution.py
+++ b/solution.py
@@ -79,7 +79,12 @@
     )
     spatial = spatial.reshape(frames_local, patches, width_local)
     columns = lax.all_to_all(spatial_out, "head", split_axis=1, concat_axis=0, tiled=True)
-    reduced = column_adder(columns, lax.all_gather(spatial, "head", axis=2, tiled=True))
+    reduced = column_adder(
+        columns,
+        jnp.concatenate(
+            lax.all_to_all(jnp.stack([spatial] * lax.axis_size("head")), "head", 0, 0), axis=2
+        ),
+    )
     stream_one = (latent.astype(jnp.float32) + local_rows[2] * reduced).astype(jnp.bfloat16)
     stream_temporal = lax.all_to_all(stream_one, "seq", split_axis=1, concat_axis=0, tiled=True)
     full_temporal = lax.all_gather(stream_temporal, "head", axis=2, tiled=True)

time: 696 us -> 666 us (0.957)
  waiting for transfers between devices: 462 us -> 424 us
    all_gather x1 -> x0, waiting for transfers between devices: 71.1 us -> none  [per_device(): lax.all_gather(spatial, 'head', axis=2, tiled=True)]
    all_to_all x0 -> x1, waiting for transfers between devices: none -> 56.4 us  [per_device(): lax.all_to_all(jnp.stack([spatial] * lax.axis_size('head')), 'head', 0, 0)]
    all_to_all x1, waiting for transfers between devices: 21.3 us -> 0.01 us  [per_device(): lax.all_to_all(spatial_out, 'head', split_axis=1, concat_axis=0, tiled=True)]
  transfers between devices with their start and end apart: 6 -> 6, of which waited for: 6 -> 5; matrix products, arithmetic and copies ran while one was open for 1% -> 7% of each run, Pallas kernels for 0% -> 0%
where the time goes in v1:
time: 666 us; the launch traced here: 657 us
  waiting for transfers between devices  424 us (64%)
  blocking collectives  93.8 us (14%)
  matrix products  73.9 us (11%)
  other arithmetic  21.1 us (3%)
  local copies, waits for them, and re-layouts  18.6 us (3%)
  between operations  13.6 us (2%)
  starting transfers between devices  11.6 us (2%)
    all_gather x1, waiting for transfers between devices, per_device(): full_two = lax.all_gather(stream_two, 'head', axis=2, tiled=True)  100 us
    all_gather x1, waiting for transfers between devices, per_device(): full_spatial = lax.all_gather(latent, 'head', axis=2, tiled=True)  97.8 us
    all_gather x1, waiting for transfers between devices, per_device(): full_temporal = lax.all_gather(stream_temporal, 'head', axis=2, tiled=True)  93.7 us
    all_gather x1, waiting for transfers between devices, per_device(): lax.all_gather(temporal, 'head', axis=2, tiled=True)  74.8 us
    all_to_all x1, waiting for transfers between devices, per_device(): lax.all_to_all(jnp.stack([spatial] * lax.axis_size('head')), 'head', 0, 0)  56.4 us
    all_to_all x1, blocking collectives, sum_at_owner(): lax.all_to_all(split_up(shard, dim, devices), axis, 0, 0, tiled=True)  52.6 us
    all_to_all x1, blocking collectives, per_device(): lax.all_to_all(temporal_out, 'head', split_axis=1, concat_axis=0, tiled=T...  24.9 us
    dot_general x2, matrix products, attend(): jnp.einsum('ghlm,gmhd->glhd', attn_weights, values, preferred_element_typ...  18.2 us
  transfers between devices with their start and end apart: 6, of which 5 were waited for; matrix products, arithmetic and copies ran while one was open for 7% of the time, Pallas kernels for 0%

profile of v1, /device:TPU:8, one launch (start us, length us, event | category | flops | bytes accessed | tf_op | source)
XLA Modules:
  0.0 656.7 jit_solution(10458745117441268103)
XLA Ops:
  6.5 0.7 all-gather.5.cloned.1.call-update
  7.3 2.3 copy.46
  9.5 5.7 all-to-all-start.1
  15.2 1.1 slice_add_fusion
  16.3 97.8 %all-gather.5.cloned.1.call-done = bf16[1,1024,2048]{2,1,0:T(8,128)(2,1)} async-done(((bf16[1,1024,256]{2,1,0:T(8,128)(2,1)}), bf16[1,1024,2048]{2,1,0:T(8,128)(2,1)}) %all-gather.5.cloned.1.call-update) | async-done | bytes 4194320 | tf_op jit(solution)/shard_map/all_gather | solution.py:68
  114.2 3.0 convert_reduce_fusion.2
  117.6 1.2 fusion.19
  118.9 1.9 fusion.33
  120.8 1.3 convolution_convert_fusion.6
  122.1 1.3 convolution_convert_fusion.5
  123.4 1.3 convolution_convert_fusion.4
  124.7 5.2 fusion.119
  129.9 8.1 %fusion.125 = f32[4,1024,1024]{1,2,0:T(8,128)} fusion(bf16[1024,4,64]{0,2,1:T(8,128)(2,1)S(1)} %bitcast.137, bf16[1024,4,64]{0,2,1:T(8,128)(2,1)S(1)} %bitcast.139), kind=kOutput, calls=%fused_computation.122 | convolution fusion | flops 536870912 | bytes 17825792 | tf_op jit(solution)/shard_map/while/body/eval_jaxpr/glhd,gmhd->ghlm/dot_general | solution.py:34
  138.0 15.7 %fusion.58 = bf16[4,64,1024]{2,1,0:T(8,128)(2,1)S(1)} fusion(bf16[1024,4,64]{0,2,1:T(8,128)(2,1)S(1)} %bitcast.157, f32[4,1024]{1,0:T(4,128)S(1)} %fusion.119, f32[4,1024,1024]{1,2,0:T(8,128)} %fusion.125), kind=kOutput, calls=%fused_computation.76 | convolution fusion | flops 558109696 | bytes 17842176 | tf_op jit(solution)/shard_map/while/body/eval_jaxpr/ghlm,gmhd->glhd/dot_general | solution.py:38
  153.7 2.5 stack.3
  156.2 5.7 all-to-all-start
  162.0 0.9 fusion.118
  162.8 0.5 copy.47
  163.4 56.4 %all-to-all-done = bf16[8,1,1024,256]{2,3,1,0:T(8,128)(2,1)} async-done(((bf16[8,1,1024,256]{2,3,1,0:T(8,128)(2,1)}), bf16[8,1,1024,256]{2,3,1,0:T(8,128)(2,1)}, u32[]{:S(2)}, u32[]{:S(2)}) %all-to-all-start) | async-done | bytes 4194336 | tf_op jit(solution)/shard_map/all_to_all | solution.py:85
  219.8 3.5 fusion.57
  223.3 0.8 copy.94
  224.1 0.5 broadcast.129
  224.6 3.8 reduce.6
  228.6 16.4 %all_to_all.60 = bf16[16,2,8192]{2,1,0:T(2,128)(2,1)S(1)} all-to-all(bf16[16,2,8192]{2,1,0:T(2,128)(2,1)S(1)} %reshape.187), channel_id=1, replica_groups=mesh['seq'=16,'head'=8] {'seq'}, dimensions={0} | all-to-all | bytes 1048576 | tf_op jit(solution)/shard_map/all_to_all | solution.py:89
  245.0 0.5 reshape.188
  245.5 0.9 copy.58
  246.6 93.7 %all-gather.7.cloned.1.call-done = bf16[16,64,2048]{2,1,0:T(8,128)(2,1)} async-done(((bf16[16,64,256]{2,1,0:T(8,128)(2,1)}), bf16[16,64,2048]{2,1,0:T(8,128)(2,1)}) %all-gather.7.cloned.1.call-update) | async-done | bytes 4194320 | tf_op jit(solution)/shard_map/all_gather | solution.py:90
  340.4 3.0 convert_reduce_fusion.1
  343.8 1.2 fusion.15
  345.0 3.0 convolution_convert_fusion.1
  348.4 4.2 convolution_convert_fusion.2
  353.1 5.0 convolution_convert_fusion.3
  358.1 2.2 reshape.176
  360.3 3.3 fusion.120
  363.6 2.5 fusion.52
  366.1 0.5 copy.53
  366.6 1.5 reshape.179
  368.2 24.9 %all_to_all.61 = bf16[256,8,256]{2,0,1:T(8,128)(2,1)S(1)} all-to-all(bf16[256,8,256]{2,0,1:T(8,128)(2,1)S(1)} %bitcast.133), channel_id=1, replica_groups=mesh['seq'=16,'head'=8] {'head'}, dimensions={1} | all-to-all | bytes 2097152 | tf_op jit(solution)/shard_map/all_to_all | solution.py:101
  393.1 74.8 %all-gather.9.cloned.1.call-done = bf16[16,64,2048]{2,1,0:T(8,128)(2,1)} async-done(((bf16[16,64,256]{2,1,0:T(8,128)(2,1)}), bf16[16,64,2048]{2,1,0:T(8,128)(2,1)}) %all-gather.9.cloned.1.call-update) | async-done | bytes 4194320 | tf_op jit(solution)/shard_map/all_gather | solution.py:102
  467.9 4.2 fusion.56
  472.2 100.4 %all-gather.11.cloned.1.call-done = bf16[16,64,2048]{2,1,0:T(8,128)(2,1)} async-done(((bf16[16,64,256]{2,1,0:T(8,128)(2,1)}), bf16[16,64,2048]{2,1,0:T(8,128)(2,1)}) %all-gather.11.cloned.1.call-update) | async-done | bytes 4194320 | tf_op jit(solution)/shard_map/all_gather | solution.py:106
  572.6 3.0 convert_reduce_fusion
  576.1 1.2 fusion.11
  577.3 15.3 %fusion.43 = bf16[16,64,2048]{2,1,0:T(8,128)(2,1)} fusion(bf16[1024,2048]{1,0:T(8,128)(2,1)} %param.15, bf16[16,64,2048]{2,1,0:T(8,128)(2,1)} %all-gather.11.cloned.1.call-done, bf16[2048,1024]{1,0:T(8,128)(2,1)} %param.14, f32[2048]{0:T(1024)S(1)} %bitcast.147, f32[2048]{0:T(1024)S(1)} %bitcast.146, f32[16,64]{1,0:T(8,128)S(1)} %add_rsqrt_fusion, ...), kind=kOutput, calls=%fused_computation.52 | convolution fusion | flops 8614051840 | bytes 16801792 | tf_op jit(solution)/shard_map/dot_general | solution.py:110
  592.6 2.8 copy.92
  595.4 52.6 %all_to_all.62 = bf16[8,16,64,256]{3,2,1,0:T(8,128)(2,1)S(1)} all-to-all(bf16[8,16,64,256]{3,2,1,0:T(8,128)(2,1)S(1)} %bitcast.128), channel_id=1, replica_groups=mesh['seq'=16,'head'=8] {'head'}, dimensions={0} | all-to-all | bytes 8388608 | tf_op jit(solution)/shard_map/all_to_all | solution.py:17
  647.9 0.7 convert_reduce_fusion.3
  649.0 0.9 add_convert_fusion
  (34 shorter events, 3.2 us)
Async XLA Ops:
  6.5 107.6 %all-gather.5.cloned.1.call-start = ((), (), s32[]{:S(2)}) async-start(), calls=%async_computation.5 | async-start | bytes 4718592 | tf_op jit(solution)/shard_map/all_gather | solution.py:68
  9.5 144.2 %all-to-all-start.1 = ((bf16[256,8,256]{0,2,1:T(8,128)(2,1)}), bf16[256,8,256]{0,2,1:T(8,128)(2,1)S(1)}, u32[]{:S(2)}, u32[]{:S(2)}) async-start(bf16[256,8,256]{0,2,1:T(8,128)(2,1)} %bitcast.16), calls=%async_computation.1 | async-start | bytes 2097152 | tf_op jit(solution)/shard_map/all_to_all | solution.py:81
  114.2 3.4 copy-start
  118.9 1.9 copy-start.7
  156.2 63.6 %copy-start.6 = (bf16[1,1024,256]{2,1,0:T(8,128)(2,1)S(1)}, bf16[1,1024,256]{2,1,0:T(8,128)(2,1)}, u32[]{:S(2)}) copy-start(bf16[1,1024,256]{2,1,0:T(8,128)(2,1)} %param.8) | copy-start | bytes 1572868
  156.2 63.6 %all-to-all-start = ((bf16[8,1,1024,256]{2,3,1,0:T(8,128)(2,1)}), bf16[8,1,1024,256]{2,3,1,0:T(8,128)(2,1)}, u32[]{:S(2)}, u32[]{:S(2)}) async-start(bf16[8,1,1024,256]{2,3,1,0:T(8,128)(2,1)} %stack.3), calls=%async_computation | async-start | bytes 8388608 | tf_op jit(solution)/shard_map/all_to_all | solution.py:85
  161.9 178.4 %all-gather.7.cloned.1.call-start = ((), (), s32[]{:S(2)}) async-start(), calls=%async_computation.6 | async-start | bytes 4718592 | tf_op jit(solution)/shard_map/all_gather | solution.py:90
  246.4 221.5 %all-gather.9.cloned.1.call-start = ((), (), s32[]{:S(2)}) async-start(), calls=%async_computation.7 | async-start | bytes 4718592 | tf_op jit(solution)/shard_map/all_gather | solution.py:102
  340.4 3.4 copy-start.1
  366.1 2.1 copy-start.5
  366.1 101.8 %copy-start.3 = (bf16[1,1024,256]{2,1,0:T(8,128)(2,1)S(1)}, bf16[1,1024,256]{2,1,0:T(8,128)(2,1)}, u32[]{:S(2)}) copy-start(bf16[1,1024,256]{2,1,0:T(8,128)(2,1)} %copy.58) | copy-start | bytes 1572868
  368.1 204.5 %all-gather.11.cloned.1.call-start = ((), (), s32[]{:S(2)}) async-start(), calls=%async_computation.8 | async-start | bytes 4718592 | tf_op jit(solution)/shard_map/all_gather | solution.py:106
  572.6 3.4 copy-start.2
  647.9 1.0 copy-start.4
Sparse Core Ops, SparseCore 0:
  8.9 105.2 all-gather.4
  246.5 93.7 all-gather.6
  368.2 99.6 all-gather.8
  472.3 100.2 all-gather.10
